TPU v7x, 32 devices: a whole 2x2x4 slice. The times are simulated.
32 devices in a mesh: blk: 8 (over y, x, core), grp: 4 (over z).
Axes of the slice: x: 2, y: 2, z: 4, core: 2. Of those that a mesh axis runs over, the one named last changes fastest.
Arguments:
- trial_vec: float32 [1536, 24], P(('blk', 'grp')), may hold values from -6 to 6
- resid_vec: float32 [1536, 24], P(('blk', 'grp')), may hold values from -6 to 6
- search_dir: float32 [1536, 24], P(('blk', 'grp')), may hold values from -6 to 6
- trial_img: float32 [1536, 24], P(('blk', 'grp')), may hold values from -12 to 12
- search_img: float32 [1536, 24], P(('blk', 'grp')), may hold values from -12 to 12
- dens_exch: bfloat16 [1536, 20480], P(('blk', 'grp')), may hold values from -0.15625 to 0.15625
- dens_direct: bfloat16 [1536, 20480], P(('blk', 'grp')), may hold values from -0.15625 to 0.15625
- screen_mat: bfloat16 [20480, 20480], P('grp', 'blk'), may hold values from -0.0390625 to 0.0390625
- coulomb: float32 [20480], replicated, may hold values from 0.2 to 2
- valence_energy: float32 [96], replicated, may hold values from -3 to -1
- conduct_energy: float32 [256], replicated, may hold values from 0.5 to 3
- valence_index: int32 [1536], P(('blk', 'grp')), may hold values from 0 to 95, as said below
- conduct_index: int32 [1536], P(('blk', 'grp')), may hold values from 0 to 255, as said below
- ritz_coef: float32 [72, 24], replicated, may hold values from -1.75 to 1.75
Outputs:
- next_trial: float32 [1536, 24], P(('blk', 'grp'))
- next_trial_img: float32 [1536, 24], P(('blk', 'grp'))
- next_search: float32 [1536, 24], P(('blk', 'grp'))
- next_search_img: float32 [1536, 24], P(('blk', 'grp'))
- gram_matrix: float32 [72, 72], replicated
Inputs may be any that keep to these rules, and one draw needn't show every extreme that they name: `valence_index`: no two pairs have both the same valence band and the same conduction band. `conduct_index`: no two pairs have both the same valence band and the same conduction band.
All inputs are finite; a program needn't handle non-finite values.
Results may differ from a plain program's by a relative error of at most 0.0034.
Values may be sent and summed in bfloat16 or wider, within the bound.
A program may use at most 64 MiB of HBM per device.

v0:
```python
import jax
import jax.numpy as jnp
from jax import lax
from jax.sharding import PartitionSpec as P


def inner_rows(left, right):
    return lax.dot_general(
        left, right, (((0,), (0,)), ((), ())), preferred_element_type=jnp.float32
    )


def exact_dot(left, right):
    return jnp.dot(left, right, precision=lax.Precision.HIGHEST)


def shards(
    trial_vec,
    resid_vec,
    search_dir,
    trial_img,
    search_img,
    dens_exch,
    dens_direct,
    screen_mat,
    coulomb,
    valence_energy,
    conduct_energy,
    valence_index,
    conduct_index,
    ritz_coef,
):
    excitons = resid_vec.shape[1]
    devices = lax.axis_size("blk") * lax.axis_size("grp")
    g_share = coulomb.shape[0] // devices
    flat_index = lax.axis_index("blk") * lax.axis_size("grp") + lax.axis_index("grp")
    own_coulomb = lax.dynamic_slice_in_dim(coulomb, flat_index * g_share, g_share, 0)
    valence_hot = (
        valence_index[:, None] == jnp.arange(valence_energy.shape[0], dtype=jnp.int32)[None, :]
    ).astype(jnp.float32)
    conduct_hot = (
        conduct_index[:, None] == jnp.arange(conduct_energy.shape[0], dtype=jnp.int32)[None, :]
    ).astype(jnp.float32)
    gap = exact_dot(conduct_hot, conduct_energy) - exact_dot(valence_hot, valence_energy)
    resid_half = resid_vec.astype(jnp.bfloat16)
    regrouped = lax.all_to_all(dens_exch, ("blk", "grp"), split_axis=1, concat_axis=0, tiled=True)
    every_resid = lax.all_gather(resid_half, ("blk", "grp"), axis=0, tiled=True)
    proj = inner_rows(regrouped, every_resid)
    weighted = (own_coulomb[:, None] * proj).astype(jnp.bfloat16)
    exch_term = lax.psum_scatter(
        jnp.dot(regrouped, weighted, preferred_element_type=jnp.float32),
        ("blk", "grp"),
        scatter_dimension=0,
        tiled=True,
    )
    block_cols = screen_mat.shape[1]
    seen_total = lax.psum(inner_rows(dens_direct, resid_half), ("blk", "grp"))
    seen = seen_total.astype(jnp.bfloat16)
    col_part = lax.dynamic_slice_in_dim(seen, lax.axis_index("blk") * block_cols, block_cols, 0)
    screen_part = jnp.dot(screen_mat, col_part, preferred_element_type=jnp.float32)
    screened = lax.psum(screen_part.astype(jnp.bfloat16), "blk")
    screened_all = lax.all_gather(screened, "grp", axis=0, tiled=True)
    direct_term = jnp.dot(dens_direct, screened_all, preferred_element_type=jnp.float32)
    resid_img = gap[:, None] * resid_vec + 2.0 * exch_term - direct_term
    basis = jnp.concatenate([trial_vec, resid_vec, search_dir], axis=1)
    images = jnp.concatenate([trial_img, resid_img, search_img], axis=1)
    local_gram = lax.dot_general(
        basis, images, (((0,), (0,)), ((), ())), precision=lax.Precision.HIGHEST
    )
    gram_matrix = lax.psum(local_gram, ("blk", "grp"))
    lower = ritz_coef[excitons:]
    next_trial = exact_dot(basis, ritz_coef)
    next_trial_img = exact_dot(images, ritz_coef)
    next_search = exact_dot(jnp.concatenate([resid_vec, search_dir], axis=1), lower)
    next_search_img = exact_dot(jnp.concatenate([resid_img, search_img], axis=1), lower)
    return (next_trial, next_trial_img, next_search, next_search_img, gram_matrix)


def solution(mesh):
    return jax.shard_map(
        shards,
        mesh=mesh,
        in_specs=(
            P(("blk", "grp"), None),
            P(("blk", "grp"), None),
            P(("blk", "grp"), None),
            P(("blk", "grp"), None),
            P(("blk", "grp"), None),
            P(("blk", "grp"), None),
            P(("blk", "grp"), None),
            P("grp", "blk"),
            P(),
            P(),
            P(),
            P(("blk", "grp")),
            P(("blk", "grp")),
            P(),
        ),
        out_specs=(
            P(("blk", "grp"), None),
            P(("blk", "grp"), None),
            P(("blk", "grp"), None),
            P(("blk", "grp"), None),
            P(),
        ),
        check_vma=False,
    )
```

profile of v0, /device:TPU:0, one launch (start us, length us, event | category | flops | bytes accessed | tf_op | source)
XLA Modules:
  0.0 329.6 jit_solution(13059465515049194300)
XLA Ops:
  8.0 3.1 copy.28
  11.1 7.4 %all-to-all-start = ((bf16[48,32,640]{2,0,1:T(8,128)(2,1)}), bf16[48,32,640]{2,0,1:T(8,128)(2,1)}, u32[]{:S(2)}, u32[]{:S(2)}) async-start(bf16[48,32,640]{2,0,1:T(8,128)(2,1)} %bitcast.42), calls=%async_computation | async-start | bytes 3932160 | tf_op jit(solution)/shard_map/all_to_all | solution.py:46
  18.6 0.0 all-reduce.3.cloned.1.call-start
  18.7 1.7 fusion.19
  20.4 77.5 %all-reduce.4 = bf16[20480,24]{0,1:T(8,128)(2,1)S(1)} all-reduce(f32[20480,24]{0,1:T(8,128)} %fusion.19), channel_id=1, replica_groups=mesh['blk'=8,'grp'=4] {'blk','grp'}, use_global_device_ids=true, to_apply=%region_1.0 | all-reduce | flops 491520 | bytes 2949120 | tf_op jit(solution)/shard_map/psum | solution.py:57
  98.0 12.7 %fusion = bf16[5120,24]{0,1:T(8,128)(2,1)} fusion(bf16[5120,2560]{1,0:T(8,128)(2,1)} %param.21, bf16[20480,24]{0,1:T(8,128)(2,1)S(1)} %all-reduce.4, s32[]{:T(128)S(6)} %select_n.7), kind=kOutput, calls=%fused_computation.1 | convolution fusion | flops 629268480 | bytes 26583044 | tf_op jit(solution)/shard_map/dot_general | solution.py:60
  110.7 0.0 reduce-scatter.4.cloned.1.call-start
  110.8 65.3 %all-gather = bf16[32,48,24]{1,2,0:T(8,128)(2,1)S(1)} all-gather(bf16[1,48,24]{1,2,0:T(8,128)(2,1)S(1)} %get-tuple-element.5), channel_id=1, replica_groups=mesh['blk'=8,'grp'=4] {'blk','grp'}, dimensions={0}, use_global_device_ids=true | all-gather | bytes 76032 | tf_op jit(solution)/shard_map/all_gather | solution.py:47
  176.2 0.3 reshape.18
  176.4 0.8 dynamic_slice.6
  177.2 0.2 convolution_bitcast_fusion.2
  177.4 0.2 fusion.3
  177.7 0.8 fusion.7
  178.5 0.8 fusion.27
  179.2 3.2 convolution_bitcast_fusion
  182.4 1.2 copy.24
  183.7 18.4 %all_gather.7 = bf16[20480,24]{0,1:T(8,128)(2,1)S(1)} all-gather(bf16[5120,24]{0,1:T(8,128)(2,1)} %all-reduce.3.cloned.1.call-done), channel_id=1, replica_groups=mesh['blk'=8,'grp'=4] {'grp'}, dimensions={0}, use_global_device_ids=true | all-gather | bytes 1228800 | tf_op jit(solution)/shard_map/all_gather | solution.py:62
  202.0 75.9 %reduce-scatter.4.cloned.1.call-done = f32[48,24]{1,0:T(8,128)} async-done(((f32[1536,24]{1,0:T(8,128)}), f32[48,24]{1,0:T(8,128)}) %reduce-scatter.4.cloned.1.call-update) | async-done | bytes 4624
  278.0 0.8 copy.25
  278.8 0.6 fusion.2
  279.4 0.8 fusion.11
  280.3 0.2 fusion.5
  280.5 0.8 fusion.6
  281.2 40.9 %psum.23 = f32[72,72]{1,0:T(8,128)} all-reduce(f32[72,72]{1,0:T(8,128)S(1)} %fusion.5), channel_id=1, replica_groups=mesh['blk'=8,'grp'=4] {'blk','grp'}, use_global_device_ids=true, to_apply=%region_3.0 | all-reduce | flops 5184 | bytes 41472 | tf_op jit(solution)/shard_map/psum | solution.py:70
  (30 shorter events, 0.2 us)
Async XLA Ops:
  8.0 10.6 %copy-start = (bf16[48,20480]{1,0:T(8,128)(2,1)S(1)}, bf16[48,20480]{1,0:T(8,128)(2,1)}, u32[]{:S(2)}) copy-start(bf16[48,20480]{1,0:T(8,128)(2,1)} %param.20) | copy-start | bytes 5898244
  11.1 7.5 %copy-start.2 = (f32[48,24]{0,1:T(8,128)S(1)}, f32[48,24]{0,1:T(8,128)}, u32[]{:S(2)}) copy-start(f32[48,24]{0,1:T(8,128)} %param.15) | copy-start | bytes 13828
  11.1 168.1 %all-to-all-start = ((bf16[48,32,640]{2,0,1:T(8,128)(2,1)}), bf16[48,32,640]{2,0,1:T(8,128)(2,1)}, u32[]{:S(2)}, u32[]{:S(2)}) async-start(bf16[48,32,640]{2,0,1:T(8,128)(2,1)} %bitcast.42), calls=%async_computation | async-start | bytes 3932160 | tf_op jit(solution)/shard_map/all_to_all | solution.py:46
  18.6 165.1 %all-reduce.3.cloned.1.call-start = ((), (), s32[]{:S(2)}) async-start(), calls=%async_computation.2 | async-start | bytes 491520 | tf_op jit(solution)/shard_map/psum | solution.py:61
  97.9 12.9 %copy-start.6 = (f32[48,24]{0,1:T(8,128)S(1)}, f32[48,24]{0,1:T(8,128)}, u32[]{:S(2)}) copy-start(f32[48,24]{0,1:T(8,128)} %param.14) | copy-start | bytes 13828
  97.9 79.3 %copy-start.4 = (f32[48,24]{0,1:T(8,128)S(1)}, f32[48,24]{0,1:T(8,128)}, u32[]{:S(2)}) copy-start(f32[48,24]{0,1:T(8,128)} %param.16) | copy-start | bytes 13828
  97.9 79.3 %copy-start.7 = (f32[256]{0:T(256)S(1)}, f32[256]{0:T(256)}, u32[]{:S(2)}) copy-start(f32[256]{0:T(256)} %param.24) | copy-start | bytes 3076
  98.0 79.3 %copy-start.8 = (s32[48]{0:T(128)S(1)}, s32[48]{0:T(128)}, u32[]{:S(2)}) copy-start(s32[48]{0:T(128)} %param.26) | copy-start | bytes 580
  98.0 79.5 %copy-start.9 = (s32[48]{0:T(128)S(1)}, s32[48]{0:T(128)}, u32[]{:S(2)}) copy-start(s32[48]{0:T(128)} %param.25) | copy-start | bytes 580
  98.0 79.5 %copy-start.10 = (f32[96]{0:T(128)S(1)}, f32[96]{0:T(128)}, u32[]{:S(2)}) copy-start(f32[96]{0:T(128)} %param.23) | copy-start | bytes 1156
  98.0 79.7 %copy-start.1 = (f32[72,24]{0,1:T(8,128)S(1)}, f32[72,24]{0,1:T(8,128)}, u32[]{:S(2)}) copy-start(f32[72,24]{0,1:T(8,128)} %param.27) | copy-start | bytes 20740
  110.7 167.3 %reduce-scatter.4.cloned.1.call-start = ((), (), s32[]{:S(2)}) async-start(), calls=%async_computation.3 | async-start | bytes 811008
  183.6 95.8 %copy-start.3 = (f32[48,24]{0,1:T(8,128)S(1)}, f32[48,24]{0,1:T(8,128)}, u32[]{:S(2)}) copy-start(f32[48,24]{0,1:T(8,128)} %param.18) | copy-start | bytes 13828
  183.6 96.6 %copy-start.5 = (f32[48,24]{0,1:T(8,128)S(1)}, f32[48,24]{0,1:T(8,128)}, u32[]{:S(2)}) copy-start(f32[48,24]{0,1:T(8,128)} %param.17) | copy-start | bytes 13828
Sparse Core Ops, SparseCore 0:
  110.8 51.7 all-reduce.2
Sparse Core Ops, SparseCore 1:
  183.7 94.2 reduce-scatter.3
where the time goes:
time: 330 us
  blocking collectives  202 us (61%)
  waiting for transfers between devices  76 us (23%)
  matrix products  22 us (7%)
  between operations  15.7 us (5%)
  starting transfers between devices  7.52 us (2%)
  local copies, waits for them, and re-layouts  6.24 us (2%)
    psum x1, blocking collectives, shards(): seen_total = lax.psum(inner_rows(dens_direct, resid_half), ('blk', 'grp'))  77.5 us
    unnamed x3, waiting for transfers between devices  76 us
    all_gather x1, blocking collectives, shards(): every_resid = lax.all_gather(resid_half, ('blk', 'grp'), axis=0, tiled=True)  65.3 us
    psum x1, blocking collectives, shards(): gram_matrix = lax.psum(local_gram, ('blk', 'grp'))  40.9 us
    all_gather x1, blocking collectives, shards(): screened_all = lax.all_gather(screened, 'grp', axis=0, tiled=True)  18.4 us
    dot_general x1, matrix products, shards(): jnp.dot(screen_mat, col_part, preferred_element_type=jnp.float32)  12.7 us
    all_to_all x1, starting transfers between devices, shards(): lax.all_to_all(dens_exch, ('blk', 'grp'), split_axis=1, concat_axis=0, ti...  7.44 us
  transfers between devices with their start and end apart: 3, of which 1 were waited for; matrix products, arithmetic and copies ran while one was open for 7% of the time, Pallas kernels for 0%

commit v1 on v0

--- a/solution.py
+++ b/solution.py
@@ -54,7 +54,9 @@
         tiled=True,
     )
     block_cols = screen_mat.shape[1]
-    seen_total = lax.psum(inner_rows(dens_direct, resid_half), ("blk", "grp"))
+    z_in = inner_rows(dens_direct, resid_half)
+    n_now = jax.lax.psum(z_in, "grp")
+    seen_total = jax.lax.psum(n_now, "blk")
     seen = seen_total.astype(jnp.bfloat16)
     col_part = lax.dynamic_slice_in_dim(seen, lax.axis_index("blk") * block_cols, block_cols, 0)
     screen_part = jnp.dot(screen_mat, col_part, preferred_element_type=jnp.float32)

time: 330 us -> 381 us (1.15)
  blocking collectives: 202 us -> 255 us
  waiting for transfers between devices: 76 us -> 71.9 us
    all_gather x1, blocking collectives: 65.3 us -> 136 us  [shards(): every_resid = lax.all_gather(resid_half, ('blk', 'grp'), axis=0, tiled=True)]
    unnamed x3 -> x4, waiting for transfers between devices: 76 us -> 26 us
    psum x1, waiting for transfers between devices: 0.02 us -> 45.9 us  [shards(): screened = lax.psum(screen_part.astype(jnp.bfloat16), 'blk')]
    psum x1, blocking collectives: 77.5 us -> 55.1 us  [shards(): seen_total = jax.lax.psum(n_now, 'blk')]
    all_gather x1, blocking collectives: 18.4 us -> 23.2 us  [shards(): screened_all = lax.all_gather(screened, 'grp', axis=0, tiled=True)]
  transfers between devices with their start and end apart: 3 -> 4, of which waited for: 1 -> 2; matrix products, arithmetic and copies ran while one was open for 7% -> 6% of each run, Pallas kernels for 0% -> 0%
where the time goes in v1:
time: 381 us; the launch traced here: 380 us
  blocking collectives  255 us (67%)
  waiting for transfers between devices  71.9 us (19%)
  matrix products  22.7 us (6%)
  between operations  15.6 us (4%)
  local copies, waits for them, and re-layouts  7.58 us (2%)
  starting transfers between devices  7.57 us (2%)
    all_gather x1, blocking collectives, shards(): every_resid = lax.all_gather(resid_half, ('blk', 'grp'), axis=0, tiled=True)  136 us
    psum x1, blocking collectives, shards(): seen_total = jax.lax.psum(n_now, 'blk')  55.1 us
    psum x1, waiting for transfers between devices, shards(): screened = lax.psum(screen_part.astype(jnp.bfloat16), 'blk')  45.9 us
    psum x1, blocking collectives, shards(): gram_matrix = lax.psum(local_gram, ('blk', 'grp'))  40.9 us
    unnamed x4, waiting for transfers between devices  26 us
    all_gather x1, blocking collectives, shards(): screened_all = lax.all_gather(screened, 'grp', axis=0, tiled=True)  23.2 us
    dot_general x1, matrix products, shards(): jnp.dot(screen_mat, col_part, preferred_element_type=jnp.float32)  12.7 us
  transfers between devices with their start and end apart: 4, of which 2 were waited for; matrix products, arithmetic and copies ran while one was open for 6% of the time, Pallas kernels for 0%

profile of v1, /device:TPU:0, one launch (start us, length us, event | category | flops | bytes accessed | tf_op | source)
XLA Modules:
  0.0 380.3 jit_solution(17788386636720532930)
XLA Ops:
  8.1 1.5 copy-done
  9.5 2.4 fusion.19
  11.9 3.0 copy.28
  15.0 7.4 %all-to-all-start = ((bf16[48,32,640]{2,0,1:T(8,128)(2,1)}), bf16[48,32,640]{2,0,1:T(8,128)(2,1)}, u32[]{:S(2)}, u32[]{:S(2)}) async-start(bf16[48,32,640]{2,0,1:T(8,128)(2,1)} %bitcast.42), calls=%async_computation | async-start | bytes 3932160 | tf_op jit(solution)/shard_map/all_to_all | solution.py:46
  22.6 135.8 %all-gather = bf16[32,48,24]{1,2,0:T(8,128)(2,1)S(1)} all-gather(bf16[1,48,24]{1,2,0:T(8,128)(2,1)S(1)} %get-tuple-element.5), channel_id=1, replica_groups=mesh['blk'=8,'grp'=4] {'blk','grp'}, dimensions={0}, use_global_device_ids=true | all-gather | bytes 76032 | tf_op jit(solution)/shard_map/all_gather | solution.py:47
  158.4 0.3 reshape.18
  158.6 0.8 dynamic_slice.6
  159.4 0.2 convolution_bitcast_fusion.2
  159.6 0.2 fusion.3
  159.8 0.9 fusion.7
  160.7 0.8 fusion.27
  161.4 55.1 %all-reduce.7 = bf16[20480,24]{0,1:T(8,128)(2,1)S(1)} all-reduce(f32[20480,24]{0,1:T(8,128)} %all-reduce.4.cloned.1.call-done), channel_id=1, replica_groups=mesh['blk'=8,'grp'=4] {'blk'}, use_global_device_ids=true, to_apply=%region_2.0 | all-reduce | flops 491520 | bytes 2949120 | tf_op jit(solution)/shard_map/psum | solution.py:59
  216.5 12.7 %fusion = bf16[5120,24]{0,1:T(8,128)(2,1)} fusion(bf16[5120,2560]{1,0:T(8,128)(2,1)} %param.21, bf16[20480,24]{0,1:T(8,128)(2,1)S(1)} %all-reduce.7, s32[]{:T(128)S(6)} %select_n.7), kind=kOutput, calls=%fused_computation.1 | convolution fusion | flops 629268480 | bytes 26583044 | tf_op jit(solution)/shard_map/dot_general | solution.py:62
  229.3 3.2 convolution_bitcast_fusion
  232.5 1.2 copy.24
  233.7 45.9 %all-reduce.6.cloned.1.call-done = bf16[5120,24]{0,1:T(8,128)(2,1)} async-done(((bf16[5120,24]{0,1:T(8,128)(2,1)}), bf16[5120,24]{0,1:T(8,128)(2,1)}) %all-reduce.6.cloned.1.call-update) | async-done | bytes 245776 | tf_op jit(solution)/shard_map/psum | solution.py:63
  279.6 23.2 %all_gather.7 = bf16[20480,24]{0,1:T(8,128)(2,1)S(1)} all-gather(bf16[5120,24]{0,1:T(8,128)(2,1)} %all-reduce.6.cloned.1.call-done), channel_id=1, replica_groups=mesh['blk'=8,'grp'=4] {'grp'}, dimensions={0}, use_global_device_ids=true | all-gather | bytes 1228800 | tf_op jit(solution)/shard_map/all_gather | solution.py:64
  302.8 26.0 %reduce-scatter.4.cloned.1.call-done = f32[48,24]{1,0:T(8,128)} async-done(((f32[1536,24]{1,0:T(8,128)}), f32[48,24]{1,0:T(8,128)}) %reduce-scatter.4.cloned.1.call-update) | async-done | bytes 4624
  328.7 0.8 copy.25
  329.5 0.6 fusion.2
  330.2 0.8 fusion.11
  331.0 0.2 fusion.5
  331.2 0.8 fusion.6
  332.0 40.9 %psum.31 = f32[72,72]{1,0:T(8,128)} all-reduce(f32[72,72]{1,0:T(8,128)S(1)} %fusion.5), channel_id=1, replica_groups=mesh['blk'=8,'grp'=4] {'blk','grp'}, use_global_device_ids=true, to_apply=%region_4.0 | all-reduce | flops 5184 | bytes 41472 | tf_op jit(solution)/shard_map/psum | solution.py:72
  (33 shorter events, 0.3 us)
Async XLA Ops:
  8.0 1.6 copy-start
  8.0 153.4 %all-reduce.4.cloned.1.call-start = ((), (), s32[]{:S(2)}) async-start(), calls=%async_computation.2 | async-start | bytes 3932160 | tf_op jit(solution)/shard_map/psum | solution.py:58
  14.9 7.6 %copy-start.6 = (f32[48,24]{0,1:T(8,128)S(1)}, f32[48,24]{0,1:T(8,128)}, u32[]{:S(2)}) copy-start(f32[48,24]{0,1:T(8,128)} %param.14) | copy-start | bytes 13828
  14.9 7.6 %copy-start.2 = (f32[48,24]{0,1:T(8,128)S(1)}, f32[48,24]{0,1:T(8,128)}, u32[]{:S(2)}) copy-start(f32[48,24]{0,1:T(8,128)} %param.15) | copy-start | bytes 13828
  14.9 144.5 %copy-start.4 = (f32[48,24]{0,1:T(8,128)S(1)}, f32[48,24]{0,1:T(8,128)}, u32[]{:S(2)}) copy-start(f32[48,24]{0,1:T(8,128)} %param.16) | copy-start | bytes 13828
  14.9 144.5 %copy-start.7 = (f32[256]{0:T(256)S(1)}, f32[256]{0:T(256)}, u32[]{:S(2)}) copy-start(f32[256]{0:T(256)} %param.24) | copy-start | bytes 3076
  14.9 144.5 %copy-start.8 = (s32[48]{0:T(128)S(1)}, s32[48]{0:T(128)}, u32[]{:S(2)}) copy-start(s32[48]{0:T(128)} %param.26) | copy-start | bytes 580
  15.0 144.6 %copy-start.9 = (s32[48]{0:T(128)S(1)}, s32[48]{0:T(128)}, u32[]{:S(2)}) copy-start(s32[48]{0:T(128)} %param.25) | copy-start | bytes 580
  15.0 144.6 %copy-start.10 = (f32[96]{0:T(128)S(1)}, f32[96]{0:T(128)}, u32[]{:S(2)}) copy-start(f32[96]{0:T(128)} %param.23) | copy-start | bytes 1156
  15.0 144.8 %copy-start.1 = (f32[72,24]{0,1:T(8,128)S(1)}, f32[72,24]{0,1:T(8,128)}, u32[]{:S(2)}) copy-start(f32[72,24]{0,1:T(8,128)} %param.27) | copy-start | bytes 20740
  15.0 214.3 %all-to-all-start = ((bf16[48,32,640]{2,0,1:T(8,128)(2,1)}), bf16[48,32,640]{2,0,1:T(8,128)(2,1)}, u32[]{:S(2)}, u32[]{:S(2)}) async-start(bf16[48,32,640]{2,0,1:T(8,128)(2,1)} %bitcast.42), calls=%async_computation | async-start | bytes 3932160 | tf_op jit(solution)/shard_map/all_to_all | solution.py:46
  22.4 257.2 %all-reduce.6.cloned.1.call-start = ((), (), s32[]{:S(2)}) async-start(), calls=%async_computation.3 | async-start | bytes 491520 | tf_op jit(solution)/shard_map/psum | solution.py:63
  229.2 99.5 %reduce-scatter.4.cloned.1.call-start = ((), (), s32[]{:S(2)}) async-start(), calls=%async_computation.4 | async-start | bytes 811008
  233.7 96.5 %copy-start.3 = (f32[48,24]{0,1:T(8,128)S(1)}, f32[48,24]{0,1:T(8,128)}, u32[]{:S(2)}) copy-start(f32[48,24]{0,1:T(8,128)} %param.18) | copy-start | bytes 13828
  233.7 97.3 %copy-start.5 = (f32[48,24]{0,1:T(8,128)S(1)}, f32[48,24]{0,1:T(8,128)}, u32[]{:S(2)}) copy-start(f32[48,24]{0,1:T(8,128)} %param.17) | copy-start | bytes 13828
Sparse Core Ops, SparseCore 0:
  12.1 122.3 all-reduce.3
  229.4 50.1 all-reduce.5
Sparse Core Ops, SparseCore 1:
  234.8 93.8 reduce-scatter.3
